TPU v7x, 32 devices: a whole 2x2x4 slice. The times are simulated.
32 devices in a mesh: row: 4 (over y, core), col: 8 (over z, x).
Axes of the slice: x: 2, y: 2, z: 4, core: 2. Of those that a mesh axis runs over, the one named last changes fastest.
Arguments:
- tokens: bfloat16 [512, 8192], P('col', 'row'), may hold values from -6 to 6
- norm_gain: float32 [8192], P('row'), may hold values from 0.1 to 1.9
- gate_weight: bfloat16 [8192, 28672], P('row', 'col'), may hold values from -0.0625 to 0.0625
- up_weight: bfloat16 [8192, 28672], P('row', 'col'), may hold values from -0.0625 to 0.0625
- down_weight: bfloat16 [28672, 8192], P('col', 'row'), may hold values from -0.03125 to 0.03125
Outputs:
- block_out: bfloat16 [512, 8192], P('col', 'row')
All inputs are finite; a program needn't handle non-finite values.
Results may differ from a plain program's by a relative error of at most 0.0017.
Values may be sent and summed in bfloat16 or wider, within the bound.
A program may use at most 128 MiB of HBM per device.

v0:
```python
import jax
import jax.numpy as jnp
from jax import lax
from jax.sharding import PartitionSpec as P

D = 8192
epsilon = 1e-05


def local(tokens, norm_gain, gate_weight, up_weight, down_weight):
    gain_row = norm_gain.astype(jnp.float32)[None, :]
    gathered = lax.all_gather(tokens, "col", axis=0, tiled=True)
    values = gathered.astype(jnp.float32)
    squares = lax.psum(jnp.sum(values * values, axis=1), "row")
    normed = (values * lax.rsqrt(squares[:, None] / D + epsilon) * gain_row).astype(jnp.bfloat16)
    gate_part = jnp.dot(normed, gate_weight, preferred_element_type=jnp.float32)
    up_part = jnp.dot(normed, up_weight, preferred_element_type=jnp.float32)
    gate_sum, up_sum = (
        lax.psum_scatter(gate_part, "row", scatter_dimension=0, tiled=True),
        lax.psum_scatter(up_part, "row", scatter_dimension=0, tiled=True),
    )
    local_hidden = (jax.nn.silu(gate_sum) * up_sum).astype(jnp.bfloat16)
    hidden = lax.all_gather(local_hidden, "row", axis=0, tiled=True)

    def down_term(length):
        row_block = lax.slice_in_dim(hidden, 0, length, axis=0)
        return jnp.dot(row_block, down_weight, preferred_element_type=jnp.float32)

    branch_out = lax.psum_scatter(
        down_term(lax.axis_size("col") * tokens.shape[0]), "col", scatter_dimension=0, tiled=True
    )
    return (tokens.astype(jnp.float32) + branch_out).astype(jnp.bfloat16)


def solution(mesh):
    placed = (P("col", "row"), P("row"), P("row", "col"), P("row", "col"), P("col", "row"))
    return jax.shard_map(
        local, mesh=mesh, in_specs=placed, out_specs=P("col", "row"), check_vma=False
    )
```

profile of v0, /device:TPU:0, one launch (start us, length us, event | category | flops | bytes accessed | tf_op | source)
XLA Modules:
  0.0 361.5 jit_solution(13591276353215433253)
XLA Ops:
  6.5 0.0 all-gather.3.cloned.1.call-start
  6.5 0.7 all-gather.3.cloned.1.call-update
  7.3 0.0 reduce-scatter.6.cloned.1.call-start
  7.3 54.0 %all-gather.3.cloned.1.call-done = bf16[512,2048]{1,0:T(8,128)(2,1)} async-done(((bf16[64,2048]{1,0:T(8,128)(2,1)}), bf16[512,2048]{1,0:T(8,128)(2,1)}) %all-gather.3.cloned.1.call-update) | async-done | bytes 2097168 | tf_op jit(solution)/shard_map/all_gather | solution.py:12
  61.3 2.1 fusion
  63.4 5.7 %psum.7 = f32[512]{0:T(512)S(1)} all-reduce(f32[512]{0:T(512)S(1)} %fusion), channel_id=1, replica_groups=mesh['row'=4,'col'=8] {'row'}, use_global_device_ids=true, to_apply=%region_1.0 | all-reduce | flops 512 | bytes 4096 | tf_op jit(solution)/shard_map/psum | solution.py:14
  69.0 13.6 %fusion.3 = f32[512,3584]{1,0:T(8,128)} fusion(bf16[2048,3584]{1,0:T(8,128)(2,1)} %param.8, bf16[512,2048]{1,0:T(8,128)(2,1)} %all-gather.3.cloned.1.call-done, f32[2048]{0:T(1024)} %param.6, f32[512]{0:T(512)S(1)} %add_rsqrt_fusion), kind=kOutput, calls=%fused_computation.6 | convolution fusion | flops 7520387072 | bytes 24127488 | tf_op jit(solution)/shard_map/dot_general | solution.py:17
  82.7 0.0 copy-start
  82.7 0.0 copy-start.2
  82.7 0.0 reduce-scatter.6.cloned.1.call-update
  82.7 0.0 reduce-scatter.4.cloned.1.call-start
  82.7 1.5 copy-done
  84.3 0.0 copy-done.2
  84.3 13.4 %fusion.5 = f32[512,3584]{1,0:T(8,128)} fusion(bf16[2048,3584]{1,0:T(8,128)(2,1)} %param.7, bf16[512,2048]{1,0:T(8,128)(2,1)S(1)} %copy-done, f32[2048]{0:T(1024)S(1)} %copy-done.2, f32[512]{0:T(512)S(1)} %add_rsqrt_fusion), kind=kOutput, calls=%fused_computation.7 | convolution fusion | flops 7520387072 | bytes 24127488 | tf_op jit(solution)/shard_map/dot_general | solution.py:16
  97.7 0.0 reduce-scatter.4.cloned.1.call-update
  97.7 0.0 all-gather.5.cloned.1.call-start
  97.8 49.8 %reduce-scatter.6.cloned.1.call-done = f32[128,3584]{1,0:T(8,128)} async-done(((f32[512,3584]{1,0:T(8,128)}), f32[128,3584]{1,0:T(8,128)}) %reduce-scatter.6.cloned.1.call-update) | async-done | bytes 1835024 | tf_op jit(solution)/shard_map/reduce_scatter | solution.py:20
  147.6 68.5 %reduce-scatter.4.cloned.1.call-done = f32[128,3584]{1,0:T(8,128)} async-done(((f32[512,3584]{1,0:T(8,128)}), f32[128,3584]{1,0:T(8,128)}) %reduce-scatter.4.cloned.1.call-update) | async-done | bytes 1835024 | tf_op jit(solution)/shard_map/reduce_scatter | solution.py:19
  216.1 3.5 multiply_convert_fusion
  219.6 0.0 all-gather.5.cloned.1.call-update
  219.6 0.0 reduce-scatter.8.cloned.1.call-start
  219.7 31.6 %all-gather.5.cloned.1.call-done = bf16[512,3584]{1,0:T(8,128)(2,1)} async-done(((bf16[128,3584]{1,0:T(8,128)(2,1)}), bf16[512,3584]{1,0:T(8,128)(2,1)}) %all-gather.5.cloned.1.call-update) | async-done | bytes 3670032 | tf_op jit(solution)/shard_map/all_gather | solution.py:23
  251.3 13.4 %fusion.7 = f32[512,2048]{1,0:T(8,128)} fusion(bf16[512,3584]{1,0:T(8,128)(2,1)} %all-gather.5.cloned.1.call-done, bf16[3584,2048]{1,0:T(8,128)(2,1)} %param.9), kind=kOutput, calls=%fused_computation.10 | convolution fusion | flops 7516192768 | bytes 22544384 | tf_op jit(solution)/shard_map/dot_general | solution.py:27
  264.7 0.0 copy-start.1
  264.7 0.0 reduce-scatter.8.cloned.1.call-update
  264.7 88.5 %reduce-scatter.8.cloned.1.call-done = f32[64,2048]{1,0:T(8,128)} async-done(((f32[512,2048]{1,0:T(8,128)}), f32[64,2048]{1,0:T(8,128)}) %reduce-scatter.8.cloned.1.call-update) | async-done | bytes 524304 | tf_op jit(solution)/shard_map/reduce_scatter | solution.py:29
  353.2 0.0 copy-done.1
  353.2 1.8 add_convert_fusion
  (1 shorter events, 0.0 us)
Async XLA Ops:
  6.5 54.8 %all-gather.3.cloned.1.call-start = ((), (), s32[]{:S(2)}) async-start(), calls=%async_computation.3 | async-start | bytes 2359296 | tf_op jit(solution)/shard_map/all_gather | solution.py:12
  7.3 140.3 %reduce-scatter.6.cloned.1.call-start = ((), (), s32[]{:S(2)}) async-start(), calls=%async_computation.5 | async-start | bytes 9175040 | tf_op jit(solution)/shard_map/reduce_scatter | solution.py:20
  82.7 1.6 copy-start
  82.7 1.6 copy-start.2
  82.7 133.4 %reduce-scatter.4.cloned.1.call-start = ((), (), s32[]{:S(2)}) async-start(), calls=%async_computation.4 | async-start | bytes 9175040 | tf_op jit(solution)/shard_map/reduce_scatter | solution.py:19
  97.7 153.6 %all-gather.5.cloned.1.call-start = ((), (), s32[]{:S(2)}) async-start(), calls=%async_computation.6 | async-start | bytes 4587520 | tf_op jit(solution)/shard_map/all_gather | solution.py:23
  219.6 133.5 %reduce-scatter.8.cloned.1.call-start = ((), (), s32[]{:S(2)}) async-start(), calls=%async_computation.7 | async-start | bytes 4718592 | tf_op jit(solution)/shard_map/reduce_scatter | solution.py:29
  264.7 88.5 %copy-start.1 = (bf16[64,2048]{1,0:T(8,128)(2,1)S(1)}, bf16[64,2048]{1,0:T(8,128)(2,1)}, u32[]{:S(2)}) copy-start(bf16[64,2048]{1,0:T(8,128)(2,1)} %param.5) | copy-start | bytes 786436
Sparse Core Ops, SparseCore 0:
  9.5 51.7 all-gather.2
  82.8 64.7 reduce-scatter.5
  150.1 65.9 reduce-scatter.3
  219.8 31.4 all-gather.4
  264.8 88.2 reduce-scatter.7
where the time goes:
time: 362 us; the launch traced here: 361 us
  waiting for transfers between devices  293 us (81%)
  matrix products  40.5 us (11%)
  between operations  13.1 us (4%)
  other arithmetic  7.36 us (2%)
  blocking collectives  5.66 us (2%)
    reduce_scatter x1, waiting for transfers between devices, local(): lax.psum_scatter(down_term(lax.axis_size('col') * tokens.shape[0]), 'col'...  88.5 us
    reduce_scatter x1, waiting for transfers between devices, local(): lax.psum_scatter(gate_part, 'row', scatter_dimension=0, tiled=True)  68.5 us
    all_gather x1, waiting for transfers between devices, local(): gathered = lax.all_gather(tokens, 'col', axis=0, tiled=True)  54 us
    reduce_scatter x1, waiting for transfers between devices, local(): lax.psum_scatter(up_part, 'row', scatter_dimension=0, tiled=True)  49.8 us
    all_gather x1, waiting for transfers between devices, local(): hidden = lax.all_gather(local_hidden, 'row', axis=0, tiled=True)  31.6 us
    dot_general x1, matrix products, local(): up_part = jnp.dot(normed, up_weight, preferred_element_type=jnp.float32)  13.6 us
    dot_general x1, matrix products, local(): gate_part = jnp.dot(normed, gate_weight, preferred_element_type=jnp.float32)  13.4 us
    dot_general x1, matrix products, down_term(): return jnp.dot(row_block, down_weight, preferred_element_type=jnp.float32)  13.4 us
  transfers between devices with their start and end apart: 5, of which 5 were waited for; matrix products, arithmetic and copies ran while one was open for 4% of the time, Pallas kernels for 0%

commit v1 on v0

--- a/solution.py
+++ b/solution.py
@@ -7,9 +7,14 @@
 epsilon = 1e-05
 
 
+def gather_by_exchange(x, axis, dim):
+    copies = jnp.concatenate([x] * lax.axis_size(axis), axis=dim)
+    return lax.all_to_all(copies, axis, dim, dim, tiled=True)
+
+
 def local(tokens, norm_gain, gate_weight, up_weight, down_weight):
     gain_row = norm_gain.astype(jnp.float32)[None, :]
-    gathered = lax.all_gather(tokens, "col", axis=0, tiled=True)
+    gathered = gather_by_exchange(tokens, "col", 0)
     values = gathered.astype(jnp.float32)
     squares = lax.psum(jnp.sum(values * values, axis=1), "row")
     normed = (values * lax.rsqrt(squares[:, None] / D + epsilon) * gain_row).astype(jnp.bfloat16)

time: 362 us -> 367 us (1.014)
  blocking collectives: 5.66 us -> 60.9 us
  waiting for transfers between devices: 293 us -> 239 us
  local copies, waits for them, and re-layouts: 1.52 us -> 7 us
    all_to_all x0 -> x1, blocking collectives: none -> 55.3 us  [gather_by_exchange(): return lax.all_to_all(copies, axis, dim, dim, tiled=True)]
    all_gather x1 -> x0, waiting for transfers between devices: 54 us -> none  [local(): gathered = lax.all_gather(tokens, 'col', axis=0, tiled=True)]
    unnamed x6 -> x15, local copies, waits for them, and re-layouts: 1.52 us -> 6.9 us
  transfers between devices with their start and end apart: 5 -> 4, of which waited for: 5 -> 4; matrix products, arithmetic and copies ran while one was open for 4% -> 4% of each run, Pallas kernels for 0% -> 0%
where the time goes in v1:
time: 367 us; the launch traced here: 366 us
  waiting for transfers between devices  239 us (65%)
  blocking collectives  60.9 us (17%)
  matrix products  39.2 us (11%)
  between operations  13.2 us (4%)
  local copies, waits for them, and re-layouts  7 us (2%)
  other arithmetic  6.3 us (2%)
    reduce_scatter x1, waiting for transfers between devices, local(): lax.psum_scatter(down_term(lax.axis_size('col') * tokens.shape[0]), 'col'...  88.5 us
    reduce_scatter x1, waiting for transfers between devices, local(): lax.psum_scatter(gate_part, 'row', scatter_dimension=0, tiled=True)  68.5 us
    all_to_all x1, blocking collectives, gather_by_exchange(): return lax.all_to_all(copies, axis, dim, dim, tiled=True)  55.3 us
    reduce_scatter x1, waiting for transfers between devices, local(): lax.psum_scatter(up_part, 'row', scatter_dimension=0, tiled=True)  50.8 us
    all_gather x1, waiting for transfers between devices, local(): hidden = lax.all_gather(local_hidden, 'row', axis=0, tiled=True)  31.6 us
    dot_general x1, matrix products, down_term(): return jnp.dot(row_block, down_weight, preferred_element_type=jnp.float32)  13.4 us
    dot_general x1, matrix products, local(): gate_part = jnp.dot(normed, gate_weight, preferred_element_type=jnp.float32)  12.9 us
    dot_general x1, matrix products, local(): up_part = jnp.dot(normed, up_weight, preferred_element_type=jnp.float32)  12.9 us
  transfers between devices with their start and end apart: 4, of which 4 were waited for; matrix products, arithmetic and copies ran while one was open for 4% of the time, Pallas kernels for 0%

profile of v1, /device:TPU:0, one launch (start us, length us, event | category | flops | bytes accessed | tf_op | source)
XLA Modules:
  0.0 366.2 jit_solution(1695974234622388195)
XLA Ops:
  6.5 0.0 copy-start
  6.5 0.0 reduce-scatter.6.cloned.1.call-start
  6.5 1.0 constant_dynamic-update-slice_fusion.7
  7.6 1.0 constant_dynamic-update-slice_fusion.6
  8.6 1.0 constant_dynamic-update-slice_fusion.5
  9.5 1.0 constant_dynamic-update-slice_fusion.4
  10.5 0.0 copy-done
  10.6 55.3 %all_to_all.9 = bf16[8,64,2048]{2,1,0:T(8,128)(2,1)S(1)} all-to-all(bf16[8,64,2048]{2,1,0:T(8,128)(2,1)S(1)} %bitcast.13), channel_id=1, replica_groups=mesh['row'=4,'col'=8] {'col'}, dimensions={0} | all-to-all | bytes 4194304 | tf_op jit(solution)/shard_map/all_to_all | solution.py:12
  65.9 0.5 multiply_reduce_fusion
  66.4 0.1 reduce_sum.12
  66.5 5.6 %psum.7 = f32[512]{0:T(512)S(1)} all-reduce(f32[512]{0:T(512)S(1)} %reduce_sum.12), channel_id=1, replica_groups=mesh['row'=4,'col'=8] {'row'}, use_global_device_ids=true, to_apply=%region_1.0 | all-reduce | flops 512 | bytes 4096 | tf_op jit(solution)/shard_map/psum | solution.py:19
  72.1 0.0 copy-done.3
  72.1 0.5 fusion.1
  72.7 0.0 copy-start.1
  72.7 1.4 copy-done.1
  74.1 12.9 %fusion.3 = f32[512,3584]{1,0:T(8,128)} fusion(bf16[512,2048]{1,0:T(8,128)(2,1)S(1)} %fusion.1, bf16[2048,3584]{1,0:T(8,128)(2,1)} %param.8), kind=kOutput, calls=%fused_computation.16 | convolution fusion | flops 7516192768 | bytes 24117248 | tf_op jit(solution)/shard_map/dot_general | solution.py:22
  87.0 0.0 reduce-scatter.6.cloned.1.call-update
  87.0 0.0 reduce-scatter.4.cloned.1.call-start
  87.0 1.5 copy-done.2
  88.6 12.9 %fusion.2 = f32[512,3584]{1,0:T(8,128)} fusion(bf16[512,2048]{1,0:T(8,128)(2,1)S(1)} %copy-done.2, bf16[2048,3584]{1,0:T(8,128)(2,1)} %param.7), kind=kOutput, calls=%fused_computation.15 | convolution fusion | flops 7516192768 | bytes 24117248 | tf_op jit(solution)/shard_map/dot_general | solution.py:21
  101.5 0.0 reduce-scatter.4.cloned.1.call-update
  101.5 0.0 all-gather.2.cloned.1.call-start
  101.5 50.8 %reduce-scatter.6.cloned.1.call-done = f32[128,3584]{1,0:T(8,128)} async-done(((f32[512,3584]{1,0:T(8,128)}), f32[128,3584]{1,0:T(8,128)}) %reduce-scatter.6.cloned.1.call-update) | async-done | bytes 1835024 | tf_op jit(solution)/shard_map/reduce_scatter | solution.py:25
  152.3 68.5 %reduce-scatter.4.cloned.1.call-done = f32[128,3584]{1,0:T(8,128)} async-done(((f32[512,3584]{1,0:T(8,128)}), f32[128,3584]{1,0:T(8,128)}) %reduce-scatter.4.cloned.1.call-update) | async-done | bytes 1835024 | tf_op jit(solution)/shard_map/reduce_scatter | solution.py:24
  220.8 3.5 multiply_convert_fusion
  224.3 0.0 all-gather.2.cloned.1.call-update
  224.3 0.0 reduce-scatter.8.cloned.1.call-start
  224.4 31.6 %all-gather.2.cloned.1.call-done = bf16[512,3584]{1,0:T(8,128)(2,1)} async-done(((bf16[128,3584]{1,0:T(8,128)(2,1)}), bf16[512,3584]{1,0:T(8,128)(2,1)}) %all-gather.2.cloned.1.call-update) | async-done | bytes 3670032 | tf_op jit(solution)/shard_map/all_gather | solution.py:28
  256.0 13.4 %fusion.4 = f32[512,2048]{1,0:T(8,128)} fusion(bf16[512,3584]{1,0:T(8,128)(2,1)} %all-gather.2.cloned.1.call-done, bf16[3584,2048]{1,0:T(8,128)(2,1)} %param.9), kind=kOutput, calls=%fused_computation.17 | convolution fusion | flops 7516192768 | bytes 22544384 | tf_op jit(solution)/shard_map/dot_general | solution.py:32
  269.4 0.0 reduce-scatter.8.cloned.1.call-update
  269.4 88.5 %reduce-scatter.8.cloned.1.call-done = f32[64,2048]{1,0:T(8,128)} async-done(((f32[512,2048]{1,0:T(8,128)}), f32[64,2048]{1,0:T(8,128)}) %reduce-scatter.8.cloned.1.call-update) | async-done | bytes 524304 | tf_op jit(solution)/shard_map/reduce_scatter | solution.py:34
  357.8 1.8 add_convert_fusion
  (7 shorter events, 0.1 us)
Async XLA Ops:
  6.5 4.0 %copy-start = (bf16[64,2048]{1,0:T(8,128)(2,1)S(1)}, bf16[64,2048]{1,0:T(8,128)(2,1)}, u32[]{:S(2)}) copy-start(bf16[64,2048]{1,0:T(8,128)(2,1)} %param.5) | copy-start | bytes 786436
  6.5 145.8 %reduce-scatter.6.cloned.1.call-start = ((), (), s32[]{:S(2)}) async-start(), calls=%async_computation.5 | async-start | bytes 9175040 | tf_op jit(solution)/shard_map/reduce_scatter | solution.py:25
  65.9 6.2 %copy-start.3 = (f32[2048]{0:T(1024)S(1)}, f32[2048]{0:T(1024)}, u32[]{:S(2)}) copy-start(f32[2048]{0:T(1024)} %param.6) | copy-start | bytes 24580
  72.7 1.4 copy-start.1
  87.0 1.6 copy-start.2
  87.0 133.9 %reduce-scatter.4.cloned.1.call-start = ((), (), s32[]{:S(2)}) async-start(), calls=%async_computation.4 | async-start | bytes 9175040 | tf_op jit(solution)/shard_map/reduce_scatter | solution.py:24
  101.5 154.5 %all-gather.2.cloned.1.call-start = ((), (), s32[]{:S(2)}) async-start(), calls=%async_computation.6 | async-start | bytes 4587520 | tf_op jit(solution)/shard_map/all_gather | solution.py:28
  224.3 133.5 %reduce-scatter.8.cloned.1.call-start = ((), (), s32[]{:S(2)}) async-start(), calls=%async_computation.7 | async-start | bytes 4718592 | tf_op jit(solution)/shard_map/reduce_scatter | solution.py:34
Sparse Core Ops, SparseCore 0:
  87.1 65.1 reduce-scatter.5
  154.9 65.9 reduce-scatter.3
  224.5 31.4 all-gather.1
  269.5 88.2 reduce-scatter.7

commit v2 on v0

--- a/solution.py
+++ b/solution.py
@@ -5,6 +5,28 @@
 
 D = 8192
 epsilon = 1e-05
+
+
+def laid_out(tiles, dim):
+    tiles = jnp.moveaxis(tiles, 0, dim)
+    shape = tiles.shape
+    return tiles.reshape(*shape[:dim], shape[dim] * shape[dim + 1], *shape[dim + 2 :])
+
+
+def doubled(x, axis):
+    size = lax.axis_size(axis)
+    blocks = x[None]
+    for level in range(size.bit_length() - 1):
+        distance = 1 << level
+        other = lax.ppermute(blocks, axis, [(i, i ^ distance) for i in range(size)])
+        both = jnp.stack([blocks, other])
+        upper = lax.axis_index(axis) >> level & 1
+        blocks = jnp.where(upper == 0, both, both[::-1]).reshape(-1, *x.shape)
+    return blocks
+
+
+def collect(array, axis, dim):
+    return laid_out(doubled(array, axis), dim)
 
 
 def local(tokens, norm_gain, gate_weight, up_weight, down_weight):
@@ -20,7 +42,7 @@
         lax.psum_scatter(up_part, "row", scatter_dimension=0, tiled=True),
     )
     local_hidden = (jax.nn.silu(gate_sum) * up_sum).astype(jnp.bfloat16)
-    hidden = lax.all_gather(local_hidden, "row", axis=0, tiled=True)
+    hidden = collect(local_hidden, "row", 0)
 
     def down_term(length):
         row_block = lax.slice_in_dim(hidden, 0, length, axis=0)

time: 362 us -> 377 us (1.041)
  waiting for transfers between devices: 293 us -> 307 us
  other arithmetic: 7.36 us -> 11.5 us
    ppermute x0 -> x2, waiting for transfers between devices: none -> 44 us  [doubled(): other = lax.ppermute(blocks, axis, [(i, i ^ distance) for i in range(size)])]
    all_gather x1 -> x0, waiting for transfers between devices: 31.6 us -> none  [local(): hidden = lax.all_gather(local_hidden, 'row', axis=0, tiled=True)]
    reduce_scatter x1, waiting for transfers between devices: 49.8 us -> 68.5 us  [local(): lax.psum_scatter(up_part, 'row', scatter_dimension=0, tiled=True)]
    reduce_scatter x1, waiting for transfers between devices: 68.5 us -> 51.8 us  [local(): lax.psum_scatter(gate_part, 'row', scatter_dimension=0, tiled=True)]
    another operation x0 -> x4, other arithmetic: none -> 4.13 us  [doubled(): both = jnp.stack([blocks, other])]
  transfers between devices with their start and end apart: 5 -> 6, of which waited for: 5 -> 6; matrix products, arithmetic and copies ran while one was open for 4% -> 4% of each run, Pallas kernels for 0% -> 0%
where the time goes in v2:
time: 377 us
  waiting for transfers between devices  307 us (81%)
  matrix products  38.4 us (10%)
  between operations  13.2 us (4%)
  other arithmetic  11.5 us (3%)
  blocking collectives  5.66 us (2%)
    reduce_scatter x1, waiting for transfers between devices, local(): lax.psum_scatter(down_term(lax.axis_size('col') * tokens.shape[0]), 'col'...  88.4 us
    reduce_scatter x1, waiting for transfers between devices, local(): lax.psum_scatter(up_part, 'row', scatter_dimension=0, tiled=True)  68.5 us
    all_gather x1, waiting for transfers between devices, local(): gathered = lax.all_gather(tokens, 'col', axis=0, tiled=True)  54 us
    reduce_scatter x1, waiting for transfers between devices, local(): lax.psum_scatter(gate_part, 'row', scatter_dimension=0, tiled=True)  51.8 us
    ppermute x2, waiting for transfers between devices, doubled(): other = lax.ppermute(blocks, axis, [(i, i ^ distance) for i in range(size)])  44 us
    dot_general x1, matrix products, local(): gate_part = jnp.dot(normed, gate_weight, preferred_element_type=jnp.float32)  13.1 us
    dot_general x1, matrix products, local(): up_part = jnp.dot(normed, up_weight, preferred_element_type=jnp.float32)  13 us
    dot_general x1, matrix products, down_term(): return jnp.dot(row_block, down_weight, preferred_element_type=jnp.float32)  12.4 us
  transfers between devices with their start and end apart: 6, of which 6 were waited for; matrix products, arithmetic and copies ran while one was open for 4% of the time, Pallas kernels for 0%

profile of v2, /device:TPU:0, one launch (start us, length us, event | category | flops | bytes accessed | tf_op | source)
XLA Modules:
  0.0 376.7 jit_solution(4605085134377526538)
XLA Ops:
  6.5 0.0 all-gather.2.cloned.1.call-start
  6.5 0.7 all-gather.2.cloned.1.call-update
  7.3 0.0 reduce-scatter.4.cloned.1.call-start
  7.3 54.0 %all-gather.2.cloned.1.call-done = bf16[512,2048]{1,0:T(8,128)(2,1)} async-done(((bf16[64,2048]{1,0:T(8,128)(2,1)}), bf16[512,2048]{1,0:T(8,128)(2,1)}) %all-gather.2.cloned.1.call-update) | async-done | bytes 2097168 | tf_op jit(solution)/shard_map/all_gather | solution.py:34
  61.3 2.2 fusion
  63.5 5.7 %psum.7 = f32[512]{0:T(512)S(1)} all-reduce(f32[512]{0:T(512)S(1)} %fusion), channel_id=1, replica_groups=mesh['row'=4,'col'=8] {'row'}, use_global_device_ids=true, to_apply=%region_1.0 | all-reduce | flops 512 | bytes 4096 | tf_op jit(solution)/shard_map/psum | solution.py:36
  69.2 0.0 copy-done.4
  69.2 0.0 copy-done.2
  69.2 13.1 %fusion.7 = f32[512,3584]{1,0:T(8,128)} fusion(bf16[2048,3584]{1,0:T(8,128)(2,1)} %param.7, bf16[512,2048]{1,0:T(8,128)(2,1)S(1)} %copy-done.2, f32[2048]{0:T(1024)S(1)} %copy-done.4, f32[512]{0:T(512)S(1)} %add_rsqrt_fusion), kind=kOutput, calls=%fused_computation.13 | convolution fusion | flops 7520387072 | bytes 24127488 | tf_op jit(solution)/shard_map/dot_general | solution.py:38
  82.3 0.0 reduce-scatter.4.cloned.1.call-update
  82.3 0.0 reduce-scatter.6.cloned.1.call-start
  82.3 13.0 %fusion.5 = f32[512,3584]{1,0:T(8,128)} fusion(bf16[2048,3584]{1,0:T(8,128)(2,1)} %param.8, bf16[512,2048]{1,0:T(8,128)(2,1)S(1)} %copy-done.2, f32[2048]{0:T(1024)S(1)} %copy-done.4, f32[512]{0:T(512)S(1)} %add_rsqrt_fusion), kind=kOutput, calls=%fused_computation.12 | convolution fusion | flops 7520387072 | bytes 24127488 | tf_op jit(solution)/shard_map/dot_general | solution.py:39
  95.3 0.0 reduce-scatter.6.cloned.1.call-update
  95.4 0.0 reduce-scatter.8.cloned.1.call-start
  95.4 51.8 %reduce-scatter.4.cloned.1.call-done = f32[128,3584]{1,0:T(8,128)} async-done(((f32[512,3584]{1,0:T(8,128)}), f32[128,3584]{1,0:T(8,128)}) %reduce-scatter.4.cloned.1.call-update) | async-done | bytes 1835024 | tf_op jit(solution)/shard_map/reduce_scatter | solution.py:41
  147.2 68.5 %reduce-scatter.6.cloned.1.call-done = f32[128,3584]{1,0:T(8,128)} async-done(((f32[512,3584]{1,0:T(8,128)}), f32[128,3584]{1,0:T(8,128)}) %reduce-scatter.6.cloned.1.call-update) | async-done | bytes 1835024 | tf_op jit(solution)/shard_map/reduce_scatter | solution.py:42
  215.7 2.7 fusion.15
  218.4 0.1 collective-permute-start
  218.5 0.0 copy-done
  218.5 0.0 copy-done.1
  218.5 0.5 fusion.14
  219.0 1.9 collective-permute-done
  221.0 0.2 pad_maximum_fusion.1
  221.1 1.6 fusion.4
  222.8 0.3 collective-permute-start.1
  223.1 42.0 %collective-permute-done.1 = bf16[2,128,3584]{2,1,0:T(8,128)(2,1)} collective-permute-done((bf16[2,128,3584]{2,1,0:T(8,128)(2,1)}, bf16[2,128,3584]{2,1,0:T(8,128)(2,1)}, u32[]{:S(2)}, u32[]{:S(2)}) %collective-permute-start.1) | collective-permute-done | bytes 1835040 | tf_op jit(solution)/shard_map/ppermute | solution.py:21
  265.1 1.8 pad_maximum_fusion
  267.0 0.6 reverse_select_fusion
  267.6 12.4 %fusion.9 = f32[512,2048]{1,0:T(8,128)} fusion(bf16[512,3584]{1,0:T(8,128)(2,1)S(1)} %bitcast.15, bf16[3584,2048]{1,0:T(8,128)(2,1)} %param.9), kind=kOutput, calls=%fused_computation.16 | convolution fusion | flops 7516192768 | bytes 22544384 | tf_op jit(solution)/shard_map/dot_general | solution.py:49
  280.0 0.0 reduce-scatter.8.cloned.1.call-update
  280.0 88.4 %reduce-scatter.8.cloned.1.call-done = f32[64,2048]{1,0:T(8,128)} async-done(((f32[512,2048]{1,0:T(8,128)}), f32[64,2048]{1,0:T(8,128)}) %reduce-scatter.8.cloned.1.call-update) | async-done | bytes 524304 | tf_op jit(solution)/shard_map/reduce_scatter | solution.py:51
  368.4 1.8 add_convert_fusion
  (7 shorter events, 0.0 us)
Async XLA Ops:
  6.5 62.7 %copy-start.4 = (f32[2048]{0:T(1024)S(1)}, f32[2048]{0:T(1024)}, u32[]{:S(2)}) copy-start(f32[2048]{0:T(1024)} %param.6) | copy-start | bytes 24580
  6.5 54.8 %all-gather.2.cloned.1.call-start = ((), (), s32[]{:S(2)}) async-start(), calls=%async_computation.3 | async-start | bytes 2359296 | tf_op jit(solution)/shard_map/all_gather | solution.py:34
  7.3 139.9 %reduce-scatter.4.cloned.1.call-start = ((), (), s32[]{:S(2)}) async-start(), calls=%async_computation.4 | async-start | bytes 9175040 | tf_op jit(solution)/shard_map/reduce_scatter | solution.py:41
  61.3 7.9 %copy-start.2 = (bf16[512,2048]{1,0:T(8,128)(2,1)S(1)}, bf16[512,2048]{1,0:T(8,128)(2,1)}, u32[]{:S(2)}) copy-start(bf16[512,2048]{1,0:T(8,128)(2,1)} %all-gather.2.cloned.1.call-done) | copy-start | bytes 6291460
  82.3 133.4 %reduce-scatter.6.cloned.1.call-start = ((), (), s32[]{:S(2)}) async-start(), calls=%async_computation.5 | async-start | bytes 9175040 | tf_op jit(solution)/shard_map/reduce_scatter | solution.py:42
  95.4 273.1 %reduce-scatter.8.cloned.1.call-start = ((), (), s32[]{:S(2)}) async-start(), calls=%async_computation.6 | async-start | bytes 4718592 | tf_op jit(solution)/shard_map/reduce_scatter | solution.py:51
  147.2 71.3 %copy-start = (f32[128,3584]{1,0:T(8,128)S(1)}, f32[128,3584]{1,0:T(8,128)}, u32[]{:S(2)}) copy-start(f32[128,3584]{1,0:T(8,128)} %reduce-scatter.4.cloned.1.call-done) | copy-start | bytes 5505028
  215.7 2.8 copy-start.1
  218.4 2.5 collective-permute-start
  222.8 42.4 %collective-permute-start.1 = (bf16[2,128,3584]{2,1,0:T(8,128)(2,1)}, bf16[2,128,3584]{2,1,0:T(8,128)(2,1)}, u32[]{:S(2)}, u32[]{:S(2)}) collective-permute-start(bf16[2,128,3584]{2,1,0:T(8,128)(2,1)} %get-tuple-element.6), channel_id=1, source_target_pairs={{0,16},{8,24},{16,0},{24,8},{1,17},{9,25},{17,1},{25,9},{2,18},{10... | collective-permute-start | bytes 5505032 | tf_op jit(solution)/shard_map/ppermute | solution.py:21
  280.0 88.5 %copy-start.3 = (bf16[64,2048]{1,0:T(8,128)(2,1)S(1)}, bf16[64,2048]{1,0:T(8,128)(2,1)}, u32[]{:S(2)}) copy-start(bf16[64,2048]{1,0:T(8,128)(2,1)} %param.5) | copy-start | bytes 786436
Sparse Core Ops, SparseCore 0:
  9.5 51.7 all-gather.1
  82.4 64.7 reduce-scatter.3
  149.7 65.9 reduce-scatter.5
  280.1 88.2 reduce-scatter.7
